TPU v7x, 32 devices: a whole 2x2x4 slice. The times are simulated.
32 devices in a mesh: grp: 4 (over y, core), loc: 8 (over z, x).
Axes of the slice: x: 2, y: 2, z: 4, core: 2. Of those that a mesh axis runs over, the one named last changes fastest.
Arguments:
- tokens: bfloat16 [8192, 1024], P(('grp', 'loc')), may hold values from -6 to 6
- w_gate: bfloat16 [32, 1024, 2816], P(('grp', 'loc')), may hold values from -0.1875 to 0.1875
- w_up: bfloat16 [32, 1024, 2816], P(('grp', 'loc')), may hold values from -0.1875 to 0.1875
- w_down: bfloat16 [32, 2816, 1024], P(('grp', 'loc')), may hold values from -0.109375 to 0.109375
- chosen: int32 [32, 128], replicated, may hold values from -1 to 8191, as said below
- gate_weights: float32 [32, 128], replicated, may hold values from 0.05 to 1
Outputs:
- combined: bfloat16 [8192, 1024], P(('grp', 'loc'))
Inputs may be any that keep to these rules, and one draw needn't show every extreme that they name: `chosen`: each entry is a token index or -1 for an empty slot, empty slots anywhere in a row. One expert's row names a token at most once. At most 8 entries of one expert's row lie among the 256 tokens of one device, and every expert has exactly 8 from some device. Some expert has no empty slot.
All inputs are finite; a program needn't handle non-finite values.
Results may differ from a plain program's by a relative error of at most 0.0085.
Values may be sent and summed in bfloat16 or wider, within the bound.
No kernel may reach another device: no remote copies, remote signals or barrier semaphores. Data moves between devices by JAX's collectives and lax.ppermute only.
A program may use at most 128 MiB of HBM per device.

v0:
```python
import jax
import jax.numpy as jnp
from jax import lax
from jax.sharding import PartitionSpec as P

PAIR_MOST = 8


def expert_apply(row_block, w_gate, w_up, w_down):
    gate_pre = jnp.dot(row_block, w_gate[0], preferred_element_type=jnp.float32)
    up_pre = jnp.dot(row_block, w_up[0], preferred_element_type=jnp.float32)
    hidden = (jax.nn.silu(gate_pre) * up_pre).astype(jnp.bfloat16)
    produced = jnp.dot(hidden, w_down[0], preferred_element_type=jnp.float32).astype(jnp.bfloat16)
    return produced


def strict_lower(length):
    row_iota = lax.broadcasted_iota(jnp.int32, (length, length), 0)
    col_iota = lax.broadcasted_iota(jnp.int32, (length, length), 1)
    return (col_iota < row_iota).astype(jnp.float32)


def compact_apply(received, chosen_row, token_count, w_gate, w_up, w_down):
    devices, slot_count, model_width = received.shape
    slot_total = chosen_row.shape[0]
    is_live = chosen_row >= 0
    source = jnp.where(is_live, chosen_row // token_count, 0)
    onehot = ((source[:, None] == jnp.arange(devices)[None, :]) & is_live[:, None]).astype(
        jnp.float32
    )
    before = jnp.dot(strict_lower(slot_total), onehot, precision=lax.Precision.HIGHEST)
    slot_rank = jnp.sum(before * onehot, axis=1).astype(jnp.int32)
    position = source * slot_count + slot_rank
    flat_iota = lax.broadcasted_iota(jnp.int32, (slot_total, devices * slot_count), 1)
    place_table = ((position[:, None] == flat_iota) & is_live[:, None]).astype(jnp.bfloat16)
    flat_rows = received.reshape(devices * slot_count, model_width)
    gathered = jnp.dot(place_table, flat_rows, preferred_element_type=jnp.float32).astype(
        jnp.bfloat16
    )
    produced = expert_apply(gathered, w_gate, w_up, w_down)
    placed = lax.dot_general(
        place_table, produced, (((0,), (0,)), ((), ())), preferred_element_type=jnp.float32
    )
    return placed.astype(jnp.bfloat16).reshape(devices, slot_count, model_width)


def shards(tokens, w_gate, w_up, w_down, chosen, gate_weights):
    local_count = lax.axis_size("loc")
    device_id = lax.axis_index("grp") * local_count + lax.axis_index("loc")
    token_count, model_width = tokens.shape
    experts, slot_total = chosen.shape
    slot_count = PAIR_MOST
    is_live = chosen >= 0
    is_mine = is_live & (chosen // token_count == device_id)
    mine_float = is_mine.astype(jnp.float32)
    slot_rank = lax.dot_general(
        mine_float,
        strict_lower(slot_total),
        (((1,), (1,)), ((), ())),
        precision=lax.Precision.HIGHEST,
    )
    rank_table = (
        (slot_rank.astype(jnp.int32)[:, :, None] == jnp.arange(slot_count)[None, None, :])
        & is_mine[:, :, None]
    ).astype(jnp.float32)
    local_index = jnp.where(is_mine, chosen - device_id * token_count, 0).astype(jnp.float32)
    pick_local = jnp.sum(rank_table * local_index[:, :, None], axis=1)
    pick_present = jnp.sum(rank_table, axis=1)
    pick_weight = jnp.sum(rank_table * gate_weights[:, :, None], axis=1)
    pick_index = jnp.where(pick_present > 0.5, pick_local.astype(jnp.int32), -1)
    token_iota = lax.broadcasted_iota(jnp.int32, (experts, slot_count, token_count), 2)
    select_table = pick_index[:, :, None] == token_iota
    outgoing = jnp.einsum(
        "ept,td->epd", select_table.astype(jnp.bfloat16), tokens, preferred_element_type=jnp.float32
    ).astype(jnp.bfloat16)
    arrived = lax.all_to_all(outgoing, ("grp", "loc"), split_axis=0, concat_axis=0, tiled=True)
    own_row = lax.dynamic_index_in_dim(chosen, device_id, 0, keepdims=False)
    produced = compact_apply(arrived, own_row, token_count, w_gate, w_up, w_down)
    returned = lax.all_to_all(produced, ("grp", "loc"), split_axis=0, concat_axis=0, tiled=True)
    mixing = (select_table.astype(jnp.float32) * pick_weight[:, :, None]).reshape(
        experts * slot_count, token_count
    )
    flat_back = returned.reshape(experts * slot_count, model_width).astype(jnp.float32)
    summed = lax.dot_general(
        mixing,
        flat_back,
        (((0,), (0,)), ((), ())),
        precision=lax.Precision.HIGHEST,
        preferred_element_type=jnp.float32,
    )
    return summed.astype(jnp.bfloat16)


def solution(mesh):
    return jax.shard_map(
        shards,
        mesh=mesh,
        in_specs=(
            P(("grp", "loc"), None),
            P(("grp", "loc"), None, None),
            P(("grp", "loc"), None, None),
            P(("grp", "loc"), None, None),
            P(),
            P(),
        ),
        out_specs=P(("grp", "loc"), None),
        check_vma=False,
    )
```

profile of v0, /device:TPU:0, one launch (start us, length us, event | category | flops | bytes accessed | tf_op | source)
XLA Modules:
  0.0 58.8 jit_solution(18383401990859371171)
XLA Ops:
  0.0 0.0 copy-start
  0.0 0.8 %select_convert_fusion = (f32[32,128]{1,0:T(8,128)S(1)}, pred[32,128]{1,0:T(32,128)(4,1)S(1)}) fusion(s32[32,128]{1,0:T(8,128)} %param.10, s32[]{:T(128)S(6)} %mul.49, s32[]{:T(128)S(6)} %add.27), kind=kLoop, calls=%fused_computation.46 | loop fusion | flops 86016 | bytes 36872 | tf_op jit(solution)/shard_map/convert_element_type | solution.py:66
  0.8 0.1 convolution_convert_fusion.3
  0.9 0.9 %select_reduce_fusion = (f32[32,8]{1,0:T(8,128)S(1)}, f32[32,8]{1,0:T(8,128)S(1)}, f32[32,8]{1,0:T(8,128)S(1)}) fusion(f32[32,128]{1,0:T(8,128)} %param.11, s32[32,128]{1,0:T(8,128)S(1)} %convolution_convert_fusion.3, pred[32,128]{1,0:T(8,128)(4,1)S(1)} %bitcast.49, f32[32,128]{1,0:T(8,128)S(1)} %get-tuple-element.8), kind=kLoop, calls=%fused_computation.27 | loop fusion | flops 261376 | bytes 56320 | tf_op jit(solution)/shard_map/reduce_sum | solution.py:69
  1.9 0.1 copy.11
  1.9 0.1 iota_compare_fusion
  2.1 0.0 copy-done
  2.1 1.1 %convolution_convert_fusion = bf16[32,8,1024]{2,1,0:T(8,128)(2,1)} fusion(bf16[256,1024]{1,0:T(8,128)(2,1)S(1)} %copy-done, pred[32,8,256]{2,0,1:T(32,128)(4,1)S(1)} %iota_compare_fusion), kind=kOutput, calls=%fused_computation.9 | convolution fusion | flops 134479872 | bytes 1114112 | tf_op jit(solution)/shard_map/ept,td->epd/dot_general | solution.py:73
  3.2 7.3 %all-to-all-start = ((bf16[32,8,1024]{2,1,0:T(8,128)(2,1)}), bf16[32,8,1024]{2,1,0:T(8,128)(2,1)S(1)}, u32[]{:S(2)}, u32[]{:S(2)}) async-start(bf16[32,8,1024]{2,1,0:T(8,128)(2,1)} %convolution_convert_fusion), calls=%async_computation | async-start | bytes 1048576 | tf_op jit(solution)/shard_map/all_to_all | solution.py:76
  10.5 0.7 %bitcast_compare_fusion = pred[128]{0:T(512)(128)(4,1)S(1)} fusion(s32[32,128]{1,0:T(8,128)} %param.10, s32[]{:T(128)S(6)} %select_n.47), kind=kLoop, calls=%fused_computation.58 | loop fusion | flops 128 | bytes 644 | tf_op jit(solution)/shard_map/ge | solution.py:26
  11.2 0.7 %fusion.42 = s32[128]{0:T(128)S(1)} fusion(s32[32,128]{1,0:T(8,128)} %param.10, s32[]{:T(128)S(6)} %select_n.47), kind=kLoop, calls=%fused_computation.60 | loop fusion | flops 2176 | bytes 1028 | tf_op jit(solution)/shard_map/jit(_where)/select_n | solution.py:27
  11.9 0.2 fusion.17
  12.1 0.7 %convert_add_fusion = s32[128]{0:T(128)S(1)} fusion(f32[128]{0:T(128)S(1)} %fusion.17, s32[32,128]{1,0:T(8,128)} %param.10, s32[]{:T(128)S(6)} %select_n.47), kind=kLoop, calls=%fused_computation.59 | loop fusion | flops 2560 | bytes 1540 | tf_op jit(solution)/shard_map/add | solution.py:33
  12.8 14.0 %all-to-all-done = bf16[32,8,1024]{2,1,0:T(8,128)(2,1)S(1)} async-done(((bf16[32,8,1024]{2,1,0:T(8,128)(2,1)}), bf16[32,8,1024]{2,1,0:T(8,128)(2,1)S(1)}, u32[]{:S(2)}, u32[]{:S(2)}) %all-to-all-start) | async-done | bytes 524320 | tf_op jit(solution)/shard_map/all_to_all | solution.py:76
  26.7 0.3 convolution_convert_fusion.2
  27.0 3.6 %fusion.4 = f32[128,2816]{1,0:T(8,128)S(1)} fusion(bf16[128,1024]{1,0:T(8,128)(2,1)S(1)} %convolution_convert_fusion.2, bf16[1,1024,2816]{2,1,0:T(8,128)(2,1)} %param.7), kind=kOutput, calls=%fused_computation.4 | convolution fusion | flops 738197504 | bytes 7471104 | tf_op jit(solution)/shard_map/dot_general | solution.py:10
  30.6 6.4 %fusion.14 = bf16[128,1024]{1,0:T(8,128)(2,1)S(1)} fusion(bf16[1,2816,1024]{2,1,0:T(8,128)(2,1)} %param.9, bf16[128,1024]{1,0:T(8,128)(2,1)S(1)} %convolution_convert_fusion.2, bf16[1,1024,2816]{2,1,0:T(8,128)(2,1)} %param.8, f32[128,2816]{1,0:T(8,128)S(1)} %fusion.4), kind=kOutput, calls=%fused_computation.13 | convolution fusion | flops 1478688768 | bytes 13500416 | tf_op jit(solution)/shard_map/dot_general | solution.py:13
  37.0 1.2 %fusion.13 = bf16[32,8,1024]{2,1,0:T(8,128)(2,1)} fusion(bf16[128,1024]{1,0:T(8,128)(2,1)S(1)} %fusion.14, s32[128]{0:T(128)S(1)} %convert_add_fusion, pred[128]{0:T(512)(128)(4,1)S(1)} %bitcast_compare_fusion), kind=kOutput, calls=%fused_computation.12 | convolution fusion | flops 67436544 | bytes 787072 | tf_op jit(solution)/shard_map/dot_general | solution.py:41
  38.2 2.6 %all-to-all-start.1 = ((bf16[32,8,1024]{2,1,0:T(8,128)(2,1)}), bf16[32,8,1024]{2,1,0:T(8,128)(2,1)S(1)}, u32[]{:S(2)}, u32[]{:S(2)}) async-start(bf16[32,8,1024]{2,1,0:T(8,128)(2,1)} %fusion.13), calls=%async_computation.1 | async-start | bytes 1048576 | tf_op jit(solution)/shard_map/all_to_all | solution.py:79
  40.8 0.1 copy.12
  40.9 16.2 %all-to-all-done.1 = bf16[32,8,1024]{2,1,0:T(8,128)(2,1)S(1)} async-done(((bf16[32,8,1024]{2,1,0:T(8,128)(2,1)}), bf16[32,8,1024]{2,1,0:T(8,128)(2,1)S(1)}, u32[]{:S(2)}, u32[]{:S(2)}) %all-to-all-start.1) | async-done | bytes 524320 | tf_op jit(solution)/shard_map/all_to_all | solution.py:79
  57.0 1.7 %fusion.12 = bf16[256,1024]{1,0:T(8,128)(2,1)} fusion(bf16[32,8,1024]{2,1,0:T(8,128)(2,1)S(1)} %all-to-all-done.1, f32[32,8]{0,1:T(8,128)S(1)} %copy.12, s32[32,8]{0,1:T(8,128)S(1)} %copy.11), kind=kOutput, calls=%fused_computation.10 | convolution fusion | flops 805699584 | bytes 1050624 | tf_op jit(solution)/shard_map/dot_general | solution.py:84
  (1 shorter events, 0.0 us)
Async XLA Ops:
  0.0 2.1 %copy-start = (bf16[256,1024]{1,0:T(8,128)(2,1)S(1)}, bf16[256,1024]{1,0:T(8,128)(2,1)}, u32[]{:S(2)}) copy-start(bf16[256,1024]{1,0:T(8,128)(2,1)} %param.6) | copy-start | bytes 1572868
  3.2 23.6 %all-to-all-start = ((bf16[32,8,1024]{2,1,0:T(8,128)(2,1)}), bf16[32,8,1024]{2,1,0:T(8,128)(2,1)S(1)}, u32[]{:S(2)}, u32[]{:S(2)}) async-start(bf16[32,8,1024]{2,1,0:T(8,128)(2,1)} %convolution_convert_fusion), calls=%async_computation | async-start | bytes 1048576 | tf_op jit(solution)/shard_map/all_to_all | solution.py:76
  38.2 18.8 %all-to-all-start.1 = ((bf16[32,8,1024]{2,1,0:T(8,128)(2,1)}), bf16[32,8,1024]{2,1,0:T(8,128)(2,1)S(1)}, u32[]{:S(2)}, u32[]{:S(2)}) async-start(bf16[32,8,1024]{2,1,0:T(8,128)(2,1)} %fusion.13), calls=%async_computation.1 | async-start | bytes 1048576 | tf_op jit(solution)/shard_map/all_to_all | solution.py:79
where the time goes:
time: 59.4 us; the launch traced here: 58.8 us
  waiting for transfers between devices  30.1 us (51%)
  matrix products  14.6 us (25%)
  starting transfers between devices  9.93 us (17%)
  other arithmetic  3.94 us (7%)
    all_to_all x1, waiting for transfers between devices, shards(): lax.all_to_all(produced, ('grp', 'loc'), split_axis=0, concat_axis=0, til...  16.2 us
    all_to_all x1, waiting for transfers between devices, shards(): lax.all_to_all(outgoing, ('grp', 'loc'), split_axis=0, concat_axis=0, til...  14 us
    all_to_all x1, starting transfers between devices, shards(): lax.all_to_all(outgoing, ('grp', 'loc'), split_axis=0, concat_axis=0, til...  7.33 us
    dot_general x1, matrix products, expert_apply(): jnp.dot(hidden, w_down[0], preferred_element_type=jnp.float32)  6.4 us
    dot_general x1, matrix products, expert_apply(): gate_pre = jnp.dot(row_block, w_gate[0], preferred_element_type=jnp.float32)  3.56 us
    all_to_all x1, starting transfers between devices, shards(): lax.all_to_all(produced, ('grp', 'loc'), split_axis=0, concat_axis=0, til...  2.61 us
    dot_general x1, matrix products, shards(): lax.dot_general(mixing, flat_back, (((0,), (0,)), ((), ())), precision=la...  1.72 us
    dot_general x1, matrix products, compact_apply(): lax.dot_general(place_table, produced, (((0,), (0,)), ((), ())), preferre...  1.2 us
  transfers between devices with their start and end apart: 2, of which 2 were waited for; matrix products, arithmetic and copies ran while one was open for 4% of the time, Pallas kernels for 0%

commit v1 on v0

v1 whole, which is shorter than its diff:
```python
import jax
import jax.numpy as jnp
from jax import lax
from jax.experimental import pallas as pl
from jax.experimental.pallas import tpu as pltpu
from jax.sharding import PartitionSpec as P

PAIR_MOST = 8
AXES = ("grp", "loc")
VMEM_SPEC = pl.BlockSpec(memory_space=pltpu.VMEM)
SMEM_SPEC = pl.BlockSpec(memory_space=pltpu.SMEM)
HBM_SPEC = pl.BlockSpec(memory_space=pltpu.HBM)


def dot(left, right):
    return jnp.dot(left, right, preferred_element_type=jnp.float32)


def ranks_of(mine):
    slots = mine.shape[1]
    row = lax.broadcasted_iota(jnp.int32, (slots, slots), 0)
    col = lax.broadcasted_iota(jnp.int32, (slots, slots), 1)
    earlier = (row < col).astype(jnp.bfloat16)
    return dot(mine.astype(jnp.bfloat16), earlier).astype(jnp.int32)


def pick_rows(device, chosen, token_count, values):
    experts, slots = chosen.shape
    local = chosen - device * token_count
    mine = (local >= 0) & (local < token_count)
    rank = jnp.where(mine, ranks_of(mine.astype(jnp.float32)), -1)
    shape = (experts, PAIR_MOST, slots)
    pair_slot = lax.broadcasted_iota(jnp.int32, shape, 1)
    hit = jnp.broadcast_to(rank[:, None, :], shape) == pair_slot
    rows = experts * PAIR_MOST

    def total(array, empty):
        spread = jnp.broadcast_to(array[:, None, :], shape)
        return jnp.sum(jnp.where(hit, spread, empty), axis=2, keepdims=True).reshape(rows, 1)

    index = total((local + 1).astype(jnp.float32), 0.0).astype(jnp.int32) - 1
    if values is None:
        return index
    return index, total(values, 0.0)


def dispatch_body(device_ref, chosen_hbm, tokens_hbm, out_ref, chosen_ref, tokens_ref, sems):
    copies = [
        pltpu.make_async_copy(chosen_hbm, chosen_ref, sems.at[0]),
        pltpu.make_async_copy(tokens_hbm, tokens_ref, sems.at[1]),
    ]
    for copy in copies:
        copy.start()
    copies[0].wait()
    token_count = tokens_ref.shape[0]
    index = pick_rows(device_ref[0], chosen_ref[...], token_count, None)
    token_iota = lax.broadcasted_iota(jnp.int32, (index.shape[0], token_count), 1)
    select = (index == token_iota).astype(jnp.bfloat16)
    copies[1].wait()
    out_ref[...] = dot(select, tokens_ref[...]).astype(jnp.bfloat16)


def table_body(device_ref, chosen_ref, weights_ref, high_ref, low_ref):
    token_count = high_ref.shape[1]
    index, weight = pick_rows(device_ref[0], chosen_ref[...], token_count, weights_ref[...])
    token_iota = lax.broadcasted_iota(jnp.int32, (index.shape[0], token_count), 1)
    table = jnp.where(index == token_iota, weight, 0.0)
    high = table.astype(jnp.bfloat16)
    high_ref[...] = high
    low_ref[...] = (table - high.astype(jnp.float32)).astype(jnp.bfloat16)


def expert_body(token_count, step, device_ref, chosen_ref, arrived_ref, gate_hbm, up_hbm, down_hbm,
                out_ref, gate_ref, up_ref, down_ref, sems):
    hidden_units = gate_ref.shape[1]
    chunks = []
    for number, start in enumerate(range(0, hidden_units, step)):
        span = pl.ds(start, min(step, hidden_units - start))
        copies = (
            pltpu.make_async_copy(gate_hbm.at[0, :, span], gate_ref.at[:, span], sems.at[0, number]),
            pltpu.make_async_copy(up_hbm.at[0, :, span], up_ref.at[:, span], sems.at[1, number]),
            pltpu.make_async_copy(down_hbm.at[0, span], down_ref.at[span], sems.at[2, number]),
        )
        for copy in copies:
            copy.start()
        chunks.append((span, copies))
    rows = arrived_ref.shape[0]
    devices = rows // PAIR_MOST
    slots = chosen_ref.shape[1]
    row = chosen_ref[pl.ds(device_ref[0], 1), :]
    first = lax.broadcasted_iota(jnp.int32, (devices, slots), 0) * token_count
    spread = jnp.broadcast_to(row, (devices, slots))
    mine = (spread >= first) & (spread < first + token_count)
    rank = jnp.where(mine, ranks_of(mine.astype(jnp.float32)), -1)
    shape = (devices, PAIR_MOST, slots)
    pair_slot = lax.broadcasted_iota(jnp.int32, shape, 1)
    hit = jnp.broadcast_to(rank[:, None, :], shape) == pair_slot
    place = jnp.where(hit, 1.0, 0.0).reshape(rows, slots).astype(jnp.bfloat16)
    block = lax.dot_general(
        place, arrived_ref[...], (((0,), (0,)), ((), ())), preferred_element_type=jnp.float32
    ).astype(jnp.bfloat16)
    total = jnp.zeros((slots, out_ref.shape[1]), jnp.float32)
    for span, (gate_copy, up_copy, down_copy) in chunks:
        gate_copy.wait()
        gate_pre = dot(block, gate_ref[:, span])
        up_copy.wait()
        up_pre = dot(block, up_ref[:, span])
        hidden = (gate_pre / (1.0 + jnp.exp(-gate_pre)) * up_pre).astype(jnp.bfloat16)
        down_copy.wait()
        total = total + dot(hidden, down_ref[span, :])
    out_ref[...] = dot(place, total.astype(jnp.bfloat16)).astype(jnp.bfloat16)


def combine_body(high_ref, low_ref, back_ref, out_ref):
    dims = (((0,), (0,)), ((), ()))
    back = back_ref[...]
    total = lax.dot_general(high_ref[...], back, dims, preferred_element_type=jnp.float32)
    total = total + lax.dot_general(low_ref[...], back, dims, preferred_element_type=jnp.float32)
    out_ref[...] = total.astype(jnp.bfloat16)


def shards(tokens, w_gate, w_up, w_down, chosen, gate_weights):
    device = lax.axis_index("grp") * lax.axis_size("loc") + lax.axis_index("loc")
    device = device.astype(jnp.int32).reshape(1)
    token_count, width = tokens.shape
    experts, _ = chosen.shape
    hidden_units = w_gate.shape[2]
    rows = experts * PAIR_MOST
    bf16 = jnp.bfloat16

    def exchange(block):
        block = block.reshape(experts, PAIR_MOST, width)
        block = lax.all_to_all(block, AXES, split_axis=0, concat_axis=0, tiled=True)
        return block.reshape(rows, width)

    small = pltpu.CompilerParams(vmem_limit_bytes=8 << 20)
    step = 512
    chunk_count = -(-hidden_units // step)

    def hbm(array):
        return pltpu.with_memory_space_constraint(array, pltpu.HBM)

    outgoing = pl.pallas_call(
        dispatch_body,
        in_specs=[SMEM_SPEC, HBM_SPEC, HBM_SPEC],
        out_specs=VMEM_SPEC,
        out_shape=jax.ShapeDtypeStruct((rows, width), bf16),
        scratch_shapes=[
            pltpu.VMEM(chosen.shape, chosen.dtype),
            pltpu.VMEM(tokens.shape, tokens.dtype),
            pltpu.SemaphoreType.DMA((2,)),
        ],
        compiler_params=small,
        name="dispatch",
    )(device, hbm(chosen), hbm(tokens))
    arrived = exchange(outgoing)
    high, low = pl.pallas_call(
        table_body,
        in_specs=[SMEM_SPEC, VMEM_SPEC, VMEM_SPEC],
        out_specs=[VMEM_SPEC] * 2,
        out_shape=[jax.ShapeDtypeStruct((rows, token_count), bf16)] * 2,
        compiler_params=small,
        cost_estimate=pl.CostEstimate(
            flops=1_000_000_000, bytes_accessed=4 * rows * token_count, transcendentals=0
        ),
        name="table",
    )(device, chosen, gate_weights)
    produced = pl.pallas_call(
        lambda *refs: expert_body(token_count, step, *refs),
        in_specs=[SMEM_SPEC] + [VMEM_SPEC] * 2 + [HBM_SPEC] * 3,
        out_specs=VMEM_SPEC,
        out_shape=jax.ShapeDtypeStruct((rows, width), bf16),
        scratch_shapes=[
            pltpu.VMEM((width, hidden_units), bf16),
            pltpu.VMEM((width, hidden_units), bf16),
            pltpu.VMEM((hidden_units, width), bf16),
            pltpu.SemaphoreType.DMA((3, chunk_count)),
        ],
        compiler_params=pltpu.CompilerParams(vmem_limit_bytes=40 << 20),
        name="expert",
    )(device, chosen, arrived, hbm(w_gate), hbm(w_up), hbm(w_down))
    returned = exchange(produced)
    return pl.pallas_call(
        combine_body,
        in_specs=[VMEM_SPEC] * 3,
        out_specs=VMEM_SPEC,
        out_shape=jax.ShapeDtypeStruct((token_count, width), bf16),
        compiler_params=small,
        name="combine",
    )(high, low, returned)


def solution(mesh):
    return jax.shard_map(
        shards,
        mesh=mesh,
        in_specs=(
            P(AXES, None),
            P(AXES, None, None),
            P(AXES, None, None),
            P(AXES, None, None),
            P(),
            P(),
        ),
        out_specs=P(AXES, None),
        check_vma=False,
    )
```

time: 59.4 us -> 54.1 us (0.911)
  blocking collectives: 0 us -> 23.4 us
  matrix products: 14.6 us -> 0 us
  waiting for transfers between devices: 30.1 us -> 15.9 us
  Pallas kernels: 0 us -> 11 us
  starting transfers between devices: 9.93 us -> 2.62 us
  other arithmetic: 3.94 us -> 0 us
    all_to_all x0 -> x1, blocking collectives: none -> 23.4 us  [exchange(): block = lax.all_to_all(block, AXES, split_axis=0, concat_axis=0, tiled=True)]
    dot_general x8 -> x0, matrix products: 14.6 us -> none  [the longest x1 6.4 us: expert_apply(): jnp.dot(hidden, w_down[0], preferred_element_type=jnp.float32)]
    all_to_all x2 -> x1, waiting for transfers between devices: 30.1 us -> 15.9 us  [exchange(): block = lax.all_to_all(block, AXES, split_axis=0, concat_axis=0, tiled=True)]
    pallas_call x0 -> x4, Pallas kernels: none -> 11 us  [the longest x1 8.02 us: shards(): pl.pallas_call(lambda *refs: expert_body(token_count, step, *refs), in_sp...]
    all_to_all x2 -> x1, starting transfers between devices: 9.93 us -> 2.62 us  [exchange(): block = lax.all_to_all(block, AXES, split_axis=0, concat_axis=0, tiled=True)]
    reduce_sum x1 -> x0, other arithmetic: 0.91 us -> none  [shards(): pick_weight = jnp.sum(rank_table * gate_weights[:, :, None], axis=1)]
    convert_element_type x1 -> x0, other arithmetic: 0.79 us -> none  [shards(): jnp.where(is_mine, chosen - device_id * token_count, 0).astype(jnp.float32)]
    unnamed x2 -> x6, local copies, waits for them, and re-layouts: 0.01 us -> 0.72 us
  transfers between devices with their start and end apart: 2 -> 1, of which waited for: 2 -> 1; matrix products, arithmetic and copies ran while one was open for 4% -> 0% of each run, Pallas kernels for 0% -> 1%
where the time goes in v1:
time: 54.1 us; the launch traced here: 53.6 us
  blocking collectives  23.4 us (43%)
  waiting for transfers between devices  15.9 us (29%)
  Pallas kernels  11 us (20%)
  starting transfers between devices  2.62 us (5%)
  local copies, waits for them, and re-layouts  0.72 us (1%)
    all_to_all x1, blocking collectives, exchange(): block = lax.all_to_all(block, AXES, split_axis=0, concat_axis=0, tiled=True)  23.4 us
    all_to_all x1, waiting for transfers between devices, exchange(): block = lax.all_to_all(block, AXES, split_axis=0, concat_axis=0, tiled=True)  15.9 us
    pallas_call x1, Pallas kernels, shards(): pl.pallas_call(lambda *refs: expert_body(token_count, step, *refs), in_sp...  8.02 us
    all_to_all x1, starting transfers between devices, exchange(): block = lax.all_to_all(block, AXES, split_axis=0, concat_axis=0, tiled=True)  2.62 us
    pallas_call x1, Pallas kernels, shards(): pl.pallas_call(dispatch_body, in_specs=[SMEM_SPEC, HBM_SPEC, HBM_SPEC], o...  1.39 us
    pallas_call x1, Pallas kernels, shards(): pl.pallas_call(combine_body, in_specs=[VMEM_SPEC] * 3, out_specs=VMEM_SPE...  1.25 us
  transfers between devices with their start and end apart: 1, of which 1 were waited for; matrix products, arithmetic and copies ran while one was open for 0% of the time, Pallas kernels for 1%

profile of v1, /device:TPU:0, one launch (start us, length us, event | category | flops | bytes accessed | tf_op | source)
XLA Modules:
  0.0 53.6 jit_solution(12983835824938651124)
XLA Ops:
  0.0 1.4 %dispatch.1 = bf16[256,1024]{1,0:T(8,128)(2,1)S(1)} custom-call(s32[1]{0:T(128)} %bitcast.device_ref.refs_0_, s32[32,128]{1,0:T(8,128)} %refs_1_.1, bf16[256,1024]{1,0:T(8,128)(2,1)} %tokens_hbm.1), custom_call_target="tpu_custom_call" | custom-call | tf_op jit(solution)/shard_map/dispatch/pallas_call | solution.py:143
  1.4 23.4 %all_to_all.10 = bf16[32,8,1024]{2,1,0:T(8,128)(2,1)S(1)} all-to-all(bf16[32,8,1024]{2,1,0:T(8,128)(2,1)S(1)} %bitcast.7), channel_id=1, replica_groups=mesh['grp'=4,'loc'=8] {'grp','loc'}, dimensions={0} | all-to-all | bytes 1048576 | tf_op jit(solution)/shard_map/all_to_all | solution.py:133
  24.8 0.0 copy-start
  24.8 0.7 %copy-done = s32[32,128]{1,0:T(8,128)S(1)} copy-done((s32[32,128]{1,0:T(8,128)S(1)}, s32[32,128]{1,0:T(8,128)}, u32[]{:S(2)}) %copy-start) | copy-done | bytes 16408
  25.5 0.0 copy-start.1
  25.5 0.0 copy-start.2
  25.5 8.0 %expert.1 = bf16[256,1024]{1,0:T(8,128)(2,1)} custom-call(s32[1]{0:T(128)} %bitcast.device_ref.refs_0_, s32[32,128]{1,0:T(8,128)S(1)} %copy-done, bf16[256,1024]{1,0:T(8,128)(2,1)S(1)} %bitcast.5, bf16[1,1024,2816]{2,1,0:T(8,128)(2,1)} %refs_3_.1, bf16[1,1024,2816]{2,1,0:T(8,128)(2,1)} %refs_4_.1, bf16[1,2816,1024]{2,1,0:T(8,128)(2,1)} %refs_5_.1), custom_call_target="tpu_custom_call" | custom-call | tf_op jit(solution)/shard_map/expert/pallas_call | solution.py:168
  33.5 2.6 %all-to-all-start.1 = ((bf16[32,8,1024]{2,1,0:T(8,128)(2,1)}), bf16[32,8,1024]{2,1,0:T(8,128)(2,1)S(1)}, u32[]{:S(2)}, u32[]{:S(2)}) async-start(bf16[32,8,1024]{2,1,0:T(8,128)(2,1)} %bitcast.3), calls=%async_computation.1 | async-start | bytes 1048576 | tf_op jit(solution)/shard_map/all_to_all | solution.py:133
  36.1 0.0 copy-done.1
  36.2 0.0 copy-done.2
  36.2 0.3 table.1
  36.5 15.9 %all-to-all-done.1 = bf16[32,8,1024]{2,1,0:T(8,128)(2,1)S(1)} async-done(((bf16[32,8,1024]{2,1,0:T(8,128)(2,1)}), bf16[32,8,1024]{2,1,0:T(8,128)(2,1)S(1)}, u32[]{:S(2)}, u32[]{:S(2)}) %all-to-all-start.1) | async-done | bytes 524320 | tf_op jit(solution)/shard_map/all_to_all | solution.py:133
  52.4 1.3 %combine.1 = bf16[256,1024]{1,0:T(8,128)(2,1)} custom-call(bf16[256,256]{1,0:T(8,128)(2,1)S(1)} %get-tuple-element.7.high_ref, bf16[256,256]{1,0:T(8,128)(2,1)S(1)} %get-tuple-element.8.low_ref, bf16[256,1024]{1,0:T(8,128)(2,1)S(1)} %bitcast.6), custom_call_target="tpu_custom_call" | custom-call | tf_op jit(solution)/shard_map/combine/pallas_call | solution.py:183
Async XLA Ops:
  24.8 0.7 %copy-start = (s32[32,128]{1,0:T(8,128)S(1)}, s32[32,128]{1,0:T(8,128)}, u32[]{:S(2)}) copy-start(s32[32,128]{1,0:T(8,128)} %refs_1_.1) | copy-start | bytes 49156
  25.5 10.7 %copy-start.1 = (s32[32,128]{1,0:T(8,128)S(1)}, s32[32,128]{1,0:T(8,128)}, u32[]{:S(2)}) copy-start(s32[32,128]{1,0:T(8,128)} %refs_1_.1) | copy-start | bytes 49156
  25.5 10.7 %copy-start.2 = (f32[32,128]{1,0:T(8,128)S(1)}, f32[32,128]{1,0:T(8,128)}, u32[]{:S(2)}) copy-start(f32[32,128]{1,0:T(8,128)} %weights_ref.1) | copy-start | bytes 49156
  33.5 18.9 %all-to-all-start.1 = ((bf16[32,8,1024]{2,1,0:T(8,128)(2,1)}), bf16[32,8,1024]{2,1,0:T(8,128)(2,1)S(1)}, u32[]{:S(2)}, u32[]{:S(2)}) async-start(bf16[32,8,1024]{2,1,0:T(8,128)(2,1)} %bitcast.3), calls=%async_computation.1 | async-start | bytes 1048576 | tf_op jit(solution)/shard_map/all_to_all | solution.py:133

commit v2 on v1

--- a/solution.py
+++ b/solution.py
@@ -60,30 +60,28 @@
     out_ref[...] = dot(select, tokens_ref[...]).astype(jnp.bfloat16)
 
 
-def table_body(device_ref, chosen_ref, weights_ref, high_ref, low_ref):
-    token_count = high_ref.shape[1]
-    index, weight = pick_rows(device_ref[0], chosen_ref[...], token_count, weights_ref[...])
-    token_iota = lax.broadcasted_iota(jnp.int32, (index.shape[0], token_count), 1)
-    table = jnp.where(index == token_iota, weight, 0.0)
-    high = table.astype(jnp.bfloat16)
-    high_ref[...] = high
-    low_ref[...] = (table - high.astype(jnp.float32)).astype(jnp.bfloat16)
-
-
-def expert_body(token_count, step, device_ref, chosen_ref, arrived_ref, gate_hbm, up_hbm, down_hbm,
-                out_ref, gate_ref, up_ref, down_ref, sems):
-    hidden_units = gate_ref.shape[1]
+def expert_body(token_count, plan, device_ref, chosen_ref, arrived_ref, weights_hbm, gate_hbm, up_hbm, down_hbm,
+                out_ref, high_ref, low_ref, weights_ref, gate_ref, up_ref, down_ref, sems, weights_sem):
+    weights_copy = pltpu.make_async_copy(weights_hbm, weights_ref, weights_sem)
     chunks = []
-    for number, start in enumerate(range(0, hidden_units, step)):
-        span = pl.ds(start, min(step, hidden_units - start))
-        copies = (
+    start = 0
+    for number, size in enumerate(plan):
+        span = pl.ds(start, size)
+        start += size
+        chunks.append((
+            span,
             pltpu.make_async_copy(gate_hbm.at[0, :, span], gate_ref.at[:, span], sems.at[0, number]),
             pltpu.make_async_copy(up_hbm.at[0, :, span], up_ref.at[:, span], sems.at[1, number]),
             pltpu.make_async_copy(down_hbm.at[0, span], down_ref.at[span], sems.at[2, number]),
-        )
-        for copy in copies:
-            copy.start()
-        chunks.append((span, copies))
+        ))
+    for number in range(len(plan) + 1):
+        if number < len(plan):
+            chunks[number][1].start()
+            chunks[number][2].start()
+        if number == 0:
+            weights_copy.start()
+        else:
+            chunks[number - 1][3].start()
     rows = arrived_ref.shape[0]
     devices = rows // PAIR_MOST
     slots = chosen_ref.shape[1]
@@ -100,15 +98,34 @@
         place, arrived_ref[...], (((0,), (0,)), ((), ())), preferred_element_type=jnp.float32
     ).astype(jnp.bfloat16)
     total = jnp.zeros((slots, out_ref.shape[1]), jnp.float32)
-    for span, (gate_copy, up_copy, down_copy) in chunks:
-        gate_copy.wait()
-        gate_pre = dot(block, gate_ref[:, span])
-        up_copy.wait()
-        up_pre = dot(block, up_ref[:, span])
-        hidden = (gate_pre / (1.0 + jnp.exp(-gate_pre)) * up_pre).astype(jnp.bfloat16)
-        down_copy.wait()
-        total = total + dot(hidden, down_ref[span, :])
+    hidden = None
+    for number in range(len(plan) + 1):
+        before = hidden
+        if number < len(plan):
+            span, gate_copy, up_copy, _ = chunks[number]
+            gate_copy.wait()
+            gate_pre = dot(block, gate_ref[:, span])
+            up_copy.wait()
+            up_pre = dot(block, up_ref[:, span])
+            hidden = (gate_pre / (1.0 + jnp.exp(-gate_pre)) * up_pre).astype(jnp.bfloat16)
+        if number == 0:
+            weights_copy.wait()
+            table(device_ref[0], chosen_ref[...], weights_ref[...], high_ref, low_ref)
+        else:
+            span, _, _, down_copy = chunks[number - 1]
+            down_copy.wait()
+            total = total + dot(before, down_ref[span, :])
     out_ref[...] = dot(place, total.astype(jnp.bfloat16)).astype(jnp.bfloat16)
+
+
+def table(device, chosen, weights, high_ref, low_ref):
+    token_count = high_ref.shape[1]
+    index, weight = pick_rows(device, chosen, token_count, weights)
+    token_iota = lax.broadcasted_iota(jnp.int32, (index.shape[0], token_count), 1)
+    full = jnp.where(index == token_iota, weight, 0.0)
+    high = full.astype(jnp.bfloat16)
+    high_ref[...] = high
+    low_ref[...] = (full - high.astype(jnp.float32)).astype(jnp.bfloat16)
 
 
 def combine_body(high_ref, low_ref, back_ref, out_ref):
@@ -134,19 +151,21 @@
         return block.reshape(rows, width)
 
     small = pltpu.CompilerParams(vmem_limit_bytes=8 << 20)
-    step = 512
-    chunk_count = -(-hidden_units // step)
+    step = 768
+    plan = [min(step, hidden_units - start) for start in range(0, hidden_units, step)]
 
     def hbm(array):
         return pltpu.with_memory_space_constraint(array, pltpu.HBM)
 
-    outgoing = pl.pallas_call(
+    outgoing, near = pl.pallas_call(
         dispatch_body,
         in_specs=[SMEM_SPEC, HBM_SPEC, HBM_SPEC],
-        out_specs=VMEM_SPEC,
-        out_shape=jax.ShapeDtypeStruct((rows, width), bf16),
+        out_specs=[VMEM_SPEC] * 2,
+        out_shape=[
+            jax.ShapeDtypeStruct((rows, width), bf16),
+            jax.ShapeDtypeStruct(chosen.shape, chosen.dtype),
+        ],
         scratch_shapes=[
-            pltpu.VMEM(chosen.shape, chosen.dtype),
             pltpu.VMEM(tokens.shape, tokens.dtype),
             pltpu.SemaphoreType.DMA((2,)),
         ],
@@ -154,31 +173,23 @@
         name="dispatch",
     )(device, hbm(chosen), hbm(tokens))
     arrived = exchange(outgoing)
-    high, low = pl.pallas_call(
-        table_body,
-        in_specs=[SMEM_SPEC, VMEM_SPEC, VMEM_SPEC],
-        out_specs=[VMEM_SPEC] * 2,
-        out_shape=[jax.ShapeDtypeStruct((rows, token_count), bf16)] * 2,
-        compiler_params=small,
-        cost_estimate=pl.CostEstimate(
-            flops=1_000_000_000, bytes_accessed=4 * rows * token_count, transcendentals=0
-        ),
-        name="table",
-    )(device, chosen, gate_weights)
-    produced = pl.pallas_call(
-        lambda *refs: expert_body(token_count, step, *refs),
-        in_specs=[SMEM_SPEC] + [VMEM_SPEC] * 2 + [HBM_SPEC] * 3,
-        out_specs=VMEM_SPEC,
-        out_shape=jax.ShapeDtypeStruct((rows, width), bf16),
+    produced, high, low = pl.pallas_call(
+        lambda *refs: expert_body(token_count, plan, *refs),
+        in_specs=[SMEM_SPEC] + [VMEM_SPEC] * 2 + [HBM_SPEC] * 4,
+        out_specs=[VMEM_SPEC] * 3,
+        out_shape=[jax.ShapeDtypeStruct((rows, width), bf16)]
+        + [jax.ShapeDtypeStruct((rows, token_count), bf16)] * 2,
         scratch_shapes=[
+            pltpu.VMEM(gate_weights.shape, gate_weights.dtype),
             pltpu.VMEM((width, hidden_units), bf16),
             pltpu.VMEM((width, hidden_units), bf16),
             pltpu.VMEM((hidden_units, width), bf16),
-            pltpu.SemaphoreType.DMA((3, chunk_count)),
+            pltpu.SemaphoreType.DMA((3, len(plan))),
+            pltpu.SemaphoreType.DMA(()),
         ],
-        compiler_params=pltpu.CompilerParams(vmem_limit_bytes=40 << 20),
+        compiler_params=pltpu.CompilerParams(vmem_limit_bytes=32 << 20),
         name="expert",
-    )(device, chosen, arrived, hbm(w_gate), hbm(w_up), hbm(w_down))
+    )(device, near, arrived, hbm(gate_weights), hbm(w_gate), hbm(w_up), hbm(w_down))
     returned = exchange(produced)
     return pl.pallas_call(
         combine_body,

time: 54.1 us -> 54.6 us (level)
  blocking collectives: 23.4 us -> 41.8 us
  waiting for transfers between devices: 15.9 us -> 0 us
  starting transfers between devices: 2.62 us -> 0 us
  Pallas kernels: 11 us -> 12.5 us
  local copies, waits for them, and re-layouts: 0.72 us -> 0 us
    all_to_all x1 -> x2, blocking collectives: 23.4 us -> 41.8 us  [exchange(): block = lax.all_to_all(block, AXES, split_axis=0, concat_axis=0, tiled=True)]
    all_to_all x1 -> x0, waiting for transfers between devices: 15.9 us -> none  [exchange(): block = lax.all_to_all(block, AXES, split_axis=0, concat_axis=0, tiled=True)]
    all_to_all x1 -> x0, starting transfers between devices: 2.62 us -> none  [exchange(): block = lax.all_to_all(block, AXES, split_axis=0, concat_axis=0, tiled=True)]
    pallas_call x2 -> x1, Pallas kernels: 8.31 us -> 9.9 us  [shards(): pl.pallas_call(lambda *refs: expert_body(token_count, plan, *refs), in_sp...]
    unnamed x6 -> x0, local copies, waits for them, and re-layouts: 0.72 us -> none
  transfers between devices with their start and end apart: 1 -> 0, of which waited for: 1 -> 0; matrix products, arithmetic and copies ran while one was open for 0% -> 0% of each run, Pallas kernels for 1% -> 0%
where the time goes in v2:
time: 54.6 us; the launch traced here: 54.3 us
  blocking collectives  41.8 us (77%)
  Pallas kernels  12.5 us (23%)
    all_to_all x2, blocking collectives, exchange(): block = lax.all_to_all(block, AXES, split_axis=0, concat_axis=0, tiled=True)  41.8 us
    pallas_call x1, Pallas kernels, shards(): pl.pallas_call(lambda *refs: expert_body(token_count, plan, *refs), in_sp...  9.9 us
    pallas_call x1, Pallas kernels, shards(): pl.pallas_call(dispatch_body, in_specs=[SMEM_SPEC, HBM_SPEC, HBM_SPEC], o...  1.39 us
    pallas_call x1, Pallas kernels, shards(): pl.pallas_call(combine_body, in_specs=[VMEM_SPEC] * 3, out_specs=VMEM_SPE...  1.26 us

profile of v2, /device:TPU:0, one launch (start us, length us, event | category | flops | bytes accessed | tf_op | source)
XLA Modules:
  0.0 54.3 jit_solution(12476498980381082310)
XLA Ops:
  0.0 1.4 %dispatch.1 = (bf16[256,1024]{1,0:T(8,128)(2,1)S(1)}, s32[32,128]{1,0:T(8,128)S(1)}) custom-call(s32[1]{0:T(128)} %bitcast.device_ref.refs_0_, s32[32,128]{1,0:T(8,128)} %chosen_hbm.1, bf16[256,1024]{1,0:T(8,128)(2,1)} %tokens_hbm.1), custom_call_target="tpu_custom_call" | custom-call | tf_op jit(solution)/shard_map/dispatch/pallas_call | solution.py:160
  1.4 23.4 %all_to_all.10 = bf16[32,8,1024]{2,1,0:T(8,128)(2,1)S(1)} all-to-all(bf16[32,8,1024]{2,1,0:T(8,128)(2,1)S(1)} %bitcast.8), channel_id=1, replica_groups=mesh['grp'=4,'loc'=8] {'grp','loc'}, dimensions={0} | all-to-all | bytes 1048576 | tf_op jit(solution)/shard_map/all_to_all | solution.py:150
  24.8 9.9 %expert.1 = (bf16[256,1024]{1,0:T(8,128)(2,1)S(1)}, bf16[256,256]{1,0:T(8,128)(2,1)S(1)}, bf16[256,256]{1,0:T(8,128)(2,1)S(1)}) custom-call(s32[1]{0:T(128)} %bitcast.device_ref.refs_0_, s32[32,128]{1,0:T(8,128)S(1)} %get-tuple-element.10.refs_1_, bf16[256,1024]{1,0:T(8,128)(2,1)S(1)} %bitcast.5, f32[32,128]{1,0:T(8,128)} %refs_3_.1, ...), custom_call_target="tpu_custom_call" | custom-call | tf_op jit(solution)/shard_map/expert/pallas_call | solution.py:176
  34.7 18.4 %all_to_all.11 = bf16[32,8,1024]{2,1,0:T(8,128)(2,1)S(1)} all-to-all(bf16[32,8,1024]{2,1,0:T(8,128)(2,1)S(1)} %bitcast.7), channel_id=1, replica_groups=mesh['grp'=4,'loc'=8] {'grp','loc'}, dimensions={0} | all-to-all | bytes 1048576 | tf_op jit(solution)/shard_map/all_to_all | solution.py:150
  53.1 1.3 %combine.1 = bf16[256,1024]{1,0:T(8,128)(2,1)} custom-call(bf16[256,256]{1,0:T(8,128)(2,1)S(1)} %get-tuple-element.12.high_ref, bf16[256,256]{1,0:T(8,128)(2,1)S(1)} %get-tuple-element.13.low_ref, bf16[256,1024]{1,0:T(8,128)(2,1)S(1)} %bitcast.6), custom_call_target="tpu_custom_call" | custom-call | tf_op jit(solution)/shard_map/combine/pallas_call | solution.py:194

commit v3 on v1

--- a/solution.py
+++ b/solution.py
@@ -39,43 +39,39 @@
         return jnp.sum(jnp.where(hit, spread, empty), axis=2, keepdims=True).reshape(rows, 1)
 
     index = total((local + 1).astype(jnp.float32), 0.0).astype(jnp.int32) - 1
-    if values is None:
-        return index
     return index, total(values, 0.0)
 
 
-def dispatch_body(device_ref, chosen_hbm, tokens_hbm, out_ref, chosen_ref, tokens_ref, sems):
+def dispatch_body(device_ref, chosen_hbm, tokens_hbm, weights_hbm, out_ref, chosen_ref, high_ref, low_ref,
+                  tokens_ref, weights_ref, sems):
     copies = [
         pltpu.make_async_copy(chosen_hbm, chosen_ref, sems.at[0]),
-        pltpu.make_async_copy(tokens_hbm, tokens_ref, sems.at[1]),
+        pltpu.make_async_copy(weights_hbm, weights_ref, sems.at[1]),
+        pltpu.make_async_copy(tokens_hbm, tokens_ref, sems.at[2]),
     ]
     for copy in copies:
         copy.start()
     copies[0].wait()
+    copies[1].wait()
     token_count = tokens_ref.shape[0]
-    index = pick_rows(device_ref[0], chosen_ref[...], token_count, None)
-    token_iota = lax.broadcasted_iota(jnp.int32, (index.shape[0], token_count), 1)
-    select = (index == token_iota).astype(jnp.bfloat16)
-    copies[1].wait()
-    out_ref[...] = dot(select, tokens_ref[...]).astype(jnp.bfloat16)
-
-
-def table_body(device_ref, chosen_ref, weights_ref, high_ref, low_ref):
-    token_count = high_ref.shape[1]
     index, weight = pick_rows(device_ref[0], chosen_ref[...], token_count, weights_ref[...])
     token_iota = lax.broadcasted_iota(jnp.int32, (index.shape[0], token_count), 1)
-    table = jnp.where(index == token_iota, weight, 0.0)
+    hit = index == token_iota
+    table = jnp.where(hit, weight, 0.0)
     high = table.astype(jnp.bfloat16)
     high_ref[...] = high
     low_ref[...] = (table - high.astype(jnp.float32)).astype(jnp.bfloat16)
+    copies[2].wait()
+    out_ref[...] = dot(hit.astype(jnp.bfloat16), tokens_ref[...]).astype(jnp.bfloat16)
 
 
-def expert_body(token_count, step, device_ref, chosen_ref, arrived_ref, gate_hbm, up_hbm, down_hbm,
+def expert_body(token_count, plan, device_ref, chosen_ref, arrived_ref, gate_hbm, up_hbm, down_hbm,
                 out_ref, gate_ref, up_ref, down_ref, sems):
-    hidden_units = gate_ref.shape[1]
     chunks = []
-    for number, start in enumerate(range(0, hidden_units, step)):
-        span = pl.ds(start, min(step, hidden_units - start))
+    start = 0
+    for number, size in enumerate(plan):
+        span = pl.ds(start, size)
+        start += size
         copies = (
             pltpu.make_async_copy(gate_hbm.at[0, :, span], gate_ref.at[:, span], sems.at[0, number]),
             pltpu.make_async_copy(up_hbm.at[0, :, span], up_ref.at[:, span], sems.at[1, number]),
@@ -134,39 +130,33 @@
         return block.reshape(rows, width)
 
     small = pltpu.CompilerParams(vmem_limit_bytes=8 << 20)
-    step = 512
-    chunk_count = -(-hidden_units // step)
+    step = 768
+    plan = [min(step, hidden_units - start) for start in range(0, hidden_units, step)]
 
     def hbm(array):
         return pltpu.with_memory_space_constraint(array, pltpu.HBM)
 
-    outgoing = pl.pallas_call(
+    outgoing, near, high, low = pl.pallas_call(
         dispatch_body,
-        in_specs=[SMEM_SPEC, HBM_SPEC, HBM_SPEC],
-        out_specs=VMEM_SPEC,
-        out_shape=jax.ShapeDtypeStruct((rows, width), bf16),
+        in_specs=[SMEM_SPEC] + [HBM_SPEC] * 3,
+        out_specs=[VMEM_SPEC] * 4,
+        out_shape=[
+            jax.ShapeDtypeStruct((rows, width), bf16),
+            jax.ShapeDtypeStruct(chosen.shape, chosen.dtype),
+            jax.ShapeDtypeStruct((rows, token_count), bf16),
+            jax.ShapeDtypeStruct((rows, token_count), bf16),
+        ],
         scratch_shapes=[
-            pltpu.VMEM(chosen.shape, chosen.dtype),
             pltpu.VMEM(tokens.shape, tokens.dtype),
-            pltpu.SemaphoreType.DMA((2,)),
+            pltpu.VMEM(gate_weights.shape, gate_weights.dtype),
+            pltpu.SemaphoreType.DMA((3,)),
         ],
         compiler_params=small,
         name="dispatch",
-    )(device, hbm(chosen), hbm(tokens))
+    )(device, hbm(chosen), hbm(tokens), hbm(gate_weights))
     arrived = exchange(outgoing)
-    high, low = pl.pallas_call(
-        table_body,
-        in_specs=[SMEM_SPEC, VMEM_SPEC, VMEM_SPEC],
-        out_specs=[VMEM_SPEC] * 2,
-        out_shape=[jax.ShapeDtypeStruct((rows, token_count), bf16)] * 2,
-        compiler_params=small,
-        cost_estimate=pl.CostEstimate(
-            flops=1_000_000_000, bytes_accessed=4 * rows * token_count, transcendentals=0
-        ),
-        name="table",
-    )(device, chosen, gate_weights)
     produced = pl.pallas_call(
-        lambda *refs: expert_body(token_count, step, *refs),
+        lambda *refs: expert_body(token_count, plan, *refs),
         in_specs=[SMEM_SPEC] + [VMEM_SPEC] * 2 + [HBM_SPEC] * 3,
         out_specs=VMEM_SPEC,
         out_shape=jax.ShapeDtypeStruct((rows, width), bf16),
@@ -174,11 +164,11 @@
             pltpu.VMEM((width, hidden_units), bf16),
             pltpu.VMEM((width, hidden_units), bf16),
             pltpu.VMEM((hidden_units, width), bf16),
-            pltpu.SemaphoreType.DMA((3, chunk_count)),
+            pltpu.SemaphoreType.DMA((3, len(plan))),
         ],
-        compiler_params=pltpu.CompilerParams(vmem_limit_bytes=40 << 20),
+        compiler_params=pltpu.CompilerParams(vmem_limit_bytes=32 << 20),
         name="expert",
-    )(device, chosen, arrived, hbm(w_gate), hbm(w_up), hbm(w_down))
+    )(device, near, arrived, hbm(w_gate), hbm(w_up), hbm(w_down))
     returned = exchange(produced)
     return pl.pallas_call(
         combine_body,

time: 54.1 us -> 51.6 us (0.954)
  blocking collectives: 23.4 us -> 41.8 us
  waiting for transfers between devices: 15.9 us -> 0 us
  starting transfers between devices: 2.62 us -> 0 us
  Pallas kernels: 11 us -> 9.55 us
  local copies, waits for them, and re-layouts: 0.72 us -> 0 us
    all_to_all x1 -> x2, blocking collectives: 23.4 us -> 41.8 us  [exchange(): block = lax.all_to_all(block, AXES, split_axis=0, concat_axis=0, tiled=True)]
    all_to_all x1 -> x0, waiting for transfers between devices: 15.9 us -> none  [exchange(): block = lax.all_to_all(block, AXES, split_axis=0, concat_axis=0, tiled=True)]
    all_to_all x1 -> x0, starting transfers between devices: 2.62 us -> none  [exchange(): block = lax.all_to_all(block, AXES, split_axis=0, concat_axis=0, tiled=True)]
    pallas_call x3 -> x2, Pallas kernels: 9.7 us -> 8.29 us  [the longest x1 6.88 us: shards(): pl.pallas_call(lambda *refs: expert_body(token_count, plan, *refs), in_sp...]
    unnamed x6 -> x0, local copies, waits for them, and re-layouts: 0.72 us -> none
  transfers between devices with their start and end apart: 1 -> 0, of which waited for: 1 -> 0; matrix products, arithmetic and copies ran while one was open for 0% -> 0% of each run, Pallas kernels for 1% -> 0%
where the time goes in v3:
time: 51.6 us; the launch traced here: 51.3 us
  blocking collectives  41.8 us (81%)
  Pallas kernels  9.55 us (19%)
    all_to_all x2, blocking collectives, exchange(): block = lax.all_to_all(block, AXES, split_axis=0, concat_axis=0, tiled=True)  41.8 us
    pallas_call x1, Pallas kernels, shards(): pl.pallas_call(lambda *refs: expert_body(token_count, plan, *refs), in_sp...  6.88 us
    pallas_call x1, Pallas kernels, shards(): pl.pallas_call(dispatch_body, in_specs=[SMEM_SPEC] + [HBM_SPEC] * 3, out_...  1.42 us
    pallas_call x1, Pallas kernels, shards(): pl.pallas_call(combine_body, in_specs=[VMEM_SPEC] * 3, out_specs=VMEM_SPE...  1.26 us

profile of v3, /device:TPU:0, one launch (start us, length us, event | category | flops | bytes accessed | tf_op | source)
XLA Modules:
  0.0 51.3 jit_solution(11824116956627821176)
XLA Ops:
  0.0 1.4 %dispatch.1 = (bf16[256,1024]{1,0:T(8,128)(2,1)S(1)}, s32[32,128]{1,0:T(8,128)S(1)}, bf16[256,256]{1,0:T(8,128)(2,1)S(1)}, bf16[256,256]{1,0:T(8,128)(2,1)S(1)}) custom-call(s32[1]{0:T(128)} %bitcast.device_ref.refs_0_, s32[32,128]{1,0:T(8,128)} %chosen_hbm.1, bf16[256,1024]{1,0:T(8,128)(2,1)} %tokens_hbm.1, f32[32,128]{1,0:T(8,128)} %weights_hbm.1), custom_call_target="tpu_custom_call" | custom-call | tf_op jit(solution)/shard_map/dispatch/pallas_call | solution.py:139
  1.4 23.4 %all_to_all.10 = bf16[32,8,1024]{2,1,0:T(8,128)(2,1)S(1)} all-to-all(bf16[32,8,1024]{2,1,0:T(8,128)(2,1)S(1)} %bitcast.8), channel_id=1, replica_groups=mesh['grp'=4,'loc'=8] {'grp','loc'}, dimensions={0} | all-to-all | bytes 1048576 | tf_op jit(solution)/shard_map/all_to_all | solution.py:129
  24.8 6.9 %expert.1 = bf16[256,1024]{1,0:T(8,128)(2,1)S(1)} custom-call(s32[1]{0:T(128)} %bitcast.device_ref.refs_0_, s32[32,128]{1,0:T(8,128)S(1)} %get-tuple-element.11.refs_1_, bf16[256,1024]{1,0:T(8,128)(2,1)S(1)} %bitcast.5, bf16[1,1024,2816]{2,1,0:T(8,128)(2,1)} %refs_3_.1, bf16[1,1024,2816]{2,1,0:T(8,128)(2,1)} %refs_4_.1, bf16[1,2816,1024]{2,1,0:T(8,128)(2,1)} %refs_5_.1), custom_call_target="tpu_custom_call" | custom-call | tf_op jit(solution)/shard_map/expert/pallas_call | solution.py:158
  31.7 18.4 %all_to_all.11 = bf16[32,8,1024]{2,1,0:T(8,128)(2,1)S(1)} all-to-all(bf16[32,8,1024]{2,1,0:T(8,128)(2,1)S(1)} %bitcast.6), channel_id=1, replica_groups=mesh['grp'=4,'loc'=8] {'grp','loc'}, dimensions={0} | all-to-all | bytes 1048576 | tf_op jit(solution)/shard_map/all_to_all | solution.py:129
  50.1 1.3 %combine.1 = bf16[256,1024]{1,0:T(8,128)(2,1)} custom-call(bf16[256,256]{1,0:T(8,128)(2,1)S(1)} %get-tuple-element.9.high_ref, bf16[256,256]{1,0:T(8,128)(2,1)S(1)} %get-tuple-element.10.low_ref, bf16[256,1024]{1,0:T(8,128)(2,1)S(1)} %bitcast.7), custom_call_target="tpu_custom_call" | custom-call | tf_op jit(solution)/shard_map/combine/pallas_call | solution.py:173

commit v4 on v3

--- a/solution.py
+++ b/solution.py
@@ -42,12 +42,14 @@
     return index, total(values, 0.0)
 
 
-def dispatch_body(device_ref, chosen_hbm, tokens_hbm, weights_hbm, out_ref, chosen_ref, high_ref, low_ref,
-                  tokens_ref, weights_ref, sems):
+def dispatch_body(device_ref, chosen_hbm, tokens_hbm, weights_hbm, gate_hbm, up_hbm,
+                  out_ref, chosen_ref, high_ref, low_ref, gate_ref, up_ref, tokens_ref, weights_ref, sems):
     copies = [
         pltpu.make_async_copy(chosen_hbm, chosen_ref, sems.at[0]),
         pltpu.make_async_copy(weights_hbm, weights_ref, sems.at[1]),
         pltpu.make_async_copy(tokens_hbm, tokens_ref, sems.at[2]),
+        pltpu.make_async_copy(gate_hbm.at[0, :, pl.ds(0, gate_ref.shape[1])], gate_ref, sems.at[3]),
+        pltpu.make_async_copy(up_hbm.at[0, :, pl.ds(0, up_ref.shape[1])], up_ref, sems.at[4]),
     ]
     for copy in copies:
         copy.start()
@@ -63,9 +65,11 @@
     low_ref[...] = (table - high.astype(jnp.float32)).astype(jnp.bfloat16)
     copies[2].wait()
     out_ref[...] = dot(hit.astype(jnp.bfloat16), tokens_ref[...]).astype(jnp.bfloat16)
-
-
-def expert_body(token_count, plan, device_ref, chosen_ref, arrived_ref, gate_hbm, up_hbm, down_hbm,
+    copies[3].wait()
+    copies[4].wait()
+
+
+def expert_body(token_count, plan, device_ref, chosen_ref, arrived_ref, gate_first, up_first, gate_hbm, up_hbm, down_hbm,
                 out_ref, gate_ref, up_ref, down_ref, sems):
     chunks = []
     start = 0
@@ -77,7 +81,7 @@
             pltpu.make_async_copy(up_hbm.at[0, :, span], up_ref.at[:, span], sems.at[1, number]),
             pltpu.make_async_copy(down_hbm.at[0, span], down_ref.at[span], sems.at[2, number]),
         )
-        for copy in copies:
+        for copy in copies if number else copies[2:]:
             copy.start()
         chunks.append((span, copies))
     rows = arrived_ref.shape[0]
@@ -96,11 +100,15 @@
         place, arrived_ref[...], (((0,), (0,)), ((), ())), preferred_element_type=jnp.float32
     ).astype(jnp.bfloat16)
     total = jnp.zeros((slots, out_ref.shape[1]), jnp.float32)
-    for span, (gate_copy, up_copy, down_copy) in chunks:
-        gate_copy.wait()
-        gate_pre = dot(block, gate_ref[:, span])
-        up_copy.wait()
-        up_pre = dot(block, up_ref[:, span])
+    for number, (span, (gate_copy, up_copy, down_copy)) in enumerate(chunks):
+        if number:
+            gate_copy.wait()
+            gate_pre = dot(block, gate_ref[:, span])
+            up_copy.wait()
+            up_pre = dot(block, up_ref[:, span])
+        else:
+            gate_pre = dot(block, gate_first[...])
+            up_pre = dot(block, up_first[...])
         hidden = (gate_pre / (1.0 + jnp.exp(-gate_pre)) * up_pre).astype(jnp.bfloat16)
         down_copy.wait()
         total = total + dot(hidden, down_ref[span, :])
@@ -136,28 +144,30 @@
     def hbm(array):
         return pltpu.with_memory_space_constraint(array, pltpu.HBM)
 
-    outgoing, near, high, low = pl.pallas_call(
+    outgoing, near, high, low, gate_first, up_first = pl.pallas_call(
         dispatch_body,
-        in_specs=[SMEM_SPEC] + [HBM_SPEC] * 3,
-        out_specs=[VMEM_SPEC] * 4,
+        in_specs=[SMEM_SPEC] + [HBM_SPEC] * 5,
+        out_specs=[VMEM_SPEC] * 6,
         out_shape=[
             jax.ShapeDtypeStruct((rows, width), bf16),
             jax.ShapeDtypeStruct(chosen.shape, chosen.dtype),
             jax.ShapeDtypeStruct((rows, token_count), bf16),
             jax.ShapeDtypeStruct((rows, token_count), bf16),
+            pltpu.VMEM((width, plan[0]), bf16),
+            pltpu.VMEM((width, plan[0]), bf16),
         ],
         scratch_shapes=[
             pltpu.VMEM(tokens.shape, tokens.dtype),
             pltpu.VMEM(gate_weights.shape, gate_weights.dtype),
-            pltpu.SemaphoreType.DMA((3,)),
+            pltpu.SemaphoreType.DMA((5,)),
         ],
         compiler_params=small,
         name="dispatch",
-    )(device, hbm(chosen), hbm(tokens), hbm(gate_weights))
+    )(device, hbm(chosen), hbm(tokens), hbm(gate_weights), hbm(w_gate), hbm(w_up))
     arrived = exchange(outgoing)
     produced = pl.pallas_call(
         lambda *refs: expert_body(token_count, plan, *refs),
-        in_specs=[SMEM_SPEC] + [VMEM_SPEC] * 2 + [HBM_SPEC] * 3,
+        in_specs=[SMEM_SPEC] + [VMEM_SPEC] * 4 + [HBM_SPEC] * 3,
         out_specs=VMEM_SPEC,
         out_shape=jax.ShapeDtypeStruct((rows, width), bf16),
         scratch_shapes=[
@@ -168,7 +178,7 @@
         ],
         compiler_params=pltpu.CompilerParams(vmem_limit_bytes=32 << 20),
         name="expert",
-    )(device, near, arrived, hbm(w_gate), hbm(w_up), hbm(w_down))
+    )(device, near, arrived, gate_first, up_first, hbm(w_gate), hbm(w_up), hbm(w_down))
     returned = exchange(produced)
     return pl.pallas_call(
         combine_body,

time: 51.6 us -> 51.9 us (level)
    pallas_call x1, Pallas kernels: 1.42 us -> 2.13 us  [shards(): pl.pallas_call(dispatch_body, in_specs=[SMEM_SPEC] + [HBM_SPEC] * 5, out_...]
where the time goes in v4:
time: 51.9 us; the launch traced here: 51.6 us
  blocking collectives  41.8 us (81%)
  Pallas kernels  9.86 us (19%)
    all_to_all x2, blocking collectives, exchange(): block = lax.all_to_all(block, AXES, split_axis=0, concat_axis=0, tiled=True)  41.8 us
    pallas_call x1, Pallas kernels, shards(): pl.pallas_call(lambda *refs: expert_body(token_count, plan, *refs), in_sp...  6.48 us
    pallas_call x1, Pallas kernels, shards(): pl.pallas_call(dispatch_body, in_specs=[SMEM_SPEC] + [HBM_SPEC] * 5, out_...  2.13 us
    pallas_call x1, Pallas kernels, shards(): pl.pallas_call(combine_body, in_specs=[VMEM_SPEC] * 3, out_specs=VMEM_SPE...  1.26 us

profile of v4, /device:TPU:0, one launch (start us, length us, event | category | flops | bytes accessed | tf_op | source)
XLA Modules:
  0.0 51.6 jit_solution(15978285448414403201)
XLA Ops:
  0.0 2.1 %dispatch.1 = (bf16[256,1024]{1,0:T(8,128)(2,1)S(1)}, s32[32,128]{1,0:T(8,128)S(1)}, bf16[256,256]{1,0:T(8,128)(2,1)S(1)}, bf16[256,256]{1,0:T(8,128)(2,1)S(1)},...) custom-call(s32[1]{0:T(128)} %bitcast.device_ref.refs_0_, s32[32,128]{1,0:T(8,128)} %chosen_hbm.1, ...), custom_call_target="tpu_custom_call" | custom-call | tf_op jit(solution)/shard_map/dispatch/pallas_call | solution.py:147
  2.1 23.4 %all_to_all.10 = bf16[32,8,1024]{2,1,0:T(8,128)(2,1)S(1)} all-to-all(bf16[32,8,1024]{2,1,0:T(8,128)(2,1)S(1)} %bitcast.8), channel_id=1, replica_groups=mesh['grp'=4,'loc'=8] {'grp','loc'}, dimensions={0} | all-to-all | bytes 1048576 | tf_op jit(solution)/shard_map/all_to_all | solution.py:137
  25.5 6.5 %expert.1 = bf16[256,1024]{1,0:T(8,128)(2,1)S(1)} custom-call(s32[1]{0:T(128)} %bitcast.device_ref.refs_0_, s32[32,128]{1,0:T(8,128)S(1)} %get-tuple-element.13.refs_1_, bf16[256,1024]{1,0:T(8,128)(2,1)S(1)} %bitcast.5, bf16[1024,768]{1,0:T(8,128)(2,1)S(1)} %get-tuple-element.15.refs_3_, bf16[1024,768]{1,0:T(8,128)(2,1)S(1)} %get-tuple-element.16.refs_4_, ...), custom_call_target="tpu_custom_call" | custom-call | tf_op jit(solution)/shard_map/expert/pallas_call | solution.py:168
  32.0 18.4 %all_to_all.11 = bf16[32,8,1024]{2,1,0:T(8,128)(2,1)S(1)} all-to-all(bf16[32,8,1024]{2,1,0:T(8,128)(2,1)S(1)} %bitcast.6), channel_id=1, replica_groups=mesh['grp'=4,'loc'=8] {'grp','loc'}, dimensions={0} | all-to-all | bytes 1048576 | tf_op jit(solution)/shard_map/all_to_all | solution.py:137
  50.4 1.3 %combine.1 = bf16[256,1024]{1,0:T(8,128)(2,1)} custom-call(bf16[256,256]{1,0:T(8,128)(2,1)S(1)} %get-tuple-element.11.high_ref, bf16[256,256]{1,0:T(8,128)(2,1)S(1)} %get-tuple-element.12.low_ref, bf16[256,1024]{1,0:T(8,128)(2,1)S(1)} %bitcast.7), custom_call_target="tpu_custom_call" | custom-call | tf_op jit(solution)/shard_map/combine/pallas_call | solution.py:183
